TPU v7x, 32 devices: a whole 2x2x4 slice. The times are simulated.
32 devices in a mesh: outer: 4 (over y, x), inner: 8 (over z, core).
Axes of the slice: x: 2, y: 2, z: 4, core: 2. Of those that a mesh axis runs over, the one named last changes fastest.
Arguments:
- ratings: bfloat16 [32768, 2048], P(('outer', 'inner')), may hold values from -4 to 4
- rating_weights: bfloat16 [32768, 2048], P(('outer', 'inner')), may hold values from 0 to 1.5, as said below
- user_counts: int32 [32768], P(('outer', 'inner')), may hold values from 16 to 96
- item_counts: int32 [8192], replicated, may hold values from 32 to 256
- users: bfloat16 [32768, 256], P(('outer', 'inner')), may hold values from -1.5 to 1.5
- user_moment: float32 [32768, 256], P(('outer', 'inner')), may hold values from -0.3 to 0.3
- items: bfloat16 [8192, 256], P(('outer', 'inner')), may hold values from -1.5 to 1.5
- item_moment: bfloat16 [8192, 256], P(('outer', 'inner')), may hold values from -0.29882812 to 0.29882812
Outputs:
- new_users: bfloat16 [32768, 256], P(('outer', 'inner'))
- new_user_moment: float32 [32768, 256], P(('outer', 'inner'))
- new_items: bfloat16 [8192, 256], P(('outer', 'inner'))
- new_item_moment: bfloat16 [8192, 256], P(('outer', 'inner'))
Inputs may be any that keep to these rules, and one draw needn't show every extreme that they name: `rating_weights`: A weight is 0 exactly where the rating is not observed, else positive.
All inputs are finite; a program needn't handle non-finite values.
Results may differ from a plain program's by a relative error of at most 0.011.
Values may be sent and summed in bfloat16 or wider, within the bound.
A program may use at most 128 MiB of HBM per device.

v0:
```python
import jax
import jax.numpy as jnp
from jax import lax
from jax.sharding import PartitionSpec as P

STEPS = 8


learn_rate = 0.3
moment_rate = 0.9
decay_rate = 0.02


def shifted(value, axis, steps):
    count = lax.axis_size(axis)
    pairs = [(source, (source + steps) % count) for source in range(count)]
    return lax.ppermute(value, axis, pairs)


def misfit_of(users, items, rated, weight):
    predicted = jnp.dot(users, items.T, preferred_element_type=jnp.float32)
    return (weight * (predicted - rated.astype(jnp.float32))).astype(jnp.bfloat16)


def item_step(misfit, users, items, moment, counts):
    product = lax.dot_general(
        misfit, users, (((0,), (0,)), ((), ())), preferred_element_type=jnp.float32
    )
    grad = product / counts[:, None] + decay_rate * items.astype(jnp.float32)
    moment_new = (moment_rate * moment.astype(jnp.float32) + grad).astype(jnp.bfloat16)
    kept = lax.optimization_barrier(moment_new)
    items_new = (items.astype(jnp.float32) - learn_rate * kept.astype(jnp.float32)).astype(
        jnp.bfloat16
    )
    return (items_new, moment_new)


def user_step(grad_sum, users, moment, counts):
    grad = grad_sum / counts[:, None] + decay_rate * users.astype(jnp.float32)
    moment_new = moment_rate * moment + grad
    users_new = (users.astype(jnp.float32) - learn_rate * moment_new).astype(jnp.bfloat16)
    return (users_new, moment_new)


def pass_block(factors, moment, step):
    if step == STEPS - 1:
        return (factors, moment)
    if step == STEPS // 2 - 1:
        return shifted((factors, moment), "outer", 1)
    return shifted((factors, moment), "inner", 1)


def body(ratings, rating_weights, user_counts, item_counts, users, user_moment, items, item_moment):
    n_outer = lax.axis_size("outer")
    n_inner = lax.axis_size("inner")
    outer_pos = lax.axis_index("outer")
    inner_pos = lax.axis_index("inner")
    block_rows = items.shape[0]
    ucount = user_counts.astype(jnp.float32)
    user_mom = user_moment
    item_mom = item_moment
    for step in range(STEPS):
        late = 1 if step >= STEPS // 2 else 0
        anchor = (outer_pos - late) % n_outer * n_inner + (inner_pos - (step - late)) % n_inner
        start = anchor * block_rows
        icount = lax.dynamic_slice_in_dim(item_counts, start, block_rows).astype(jnp.float32)
        rated = ratings[:, step * block_rows : (step + 1) * block_rows]
        weight = rating_weights[:, step * block_rows : (step + 1) * block_rows].astype(jnp.float32)
        misfit = misfit_of(users, items, rated, weight)
        grad_sum = jnp.dot(misfit, items, preferred_element_type=jnp.float32)
        new_items, new_imom = item_step(misfit, users, items, item_mom, icount)
        users, user_mom = user_step(grad_sum, users, user_mom, ucount)
        items, item_mom = pass_block(new_items, new_imom, step)
    return (users, user_mom, items, item_mom)


def solution(mesh):
    in_specs = (
        P(("outer", "inner"), None),
        P(("outer", "inner"), None),
        P(("outer", "inner")),
        P(),
        P(("outer", "inner"), None),
        P(("outer", "inner"), None),
        P(("outer", "inner"), None),
        P(("outer", "inner"), None),
    )
    out_specs = (
        P(("outer", "inner"), None),
        P(("outer", "inner"), None),
        P(("outer", "inner"), None),
        P(("outer", "inner"), None),
    )
    return jax.shard_map(body, mesh=mesh, in_specs=in_specs, out_specs=out_specs, check_vma=False)
```

profile of v0, /device:TPU:0, one launch (start us, length us, event | category | flops | bytes accessed | tf_op | source)
XLA Modules:
  0.0 68.2 jit_solution(12247817347069057251)
XLA Ops:
  0.6 0.0 copy-start.6
  0.6 0.0 copy-start.1
  0.8 1.9 %fusion.18 = bf16[1024,256]{1,0:T(8,128)(2,1)S(1)} fusion(bf16[1024,256]{1,0:T(8,128)(2,1)} %param.12, bf16[256,256]{1,0:T(8,128)(2,1)} %param.14, bf16[1024,2048]{1,0:T(8,128)(2,1)} %param.8, bf16[1024,2048]{1,0:T(8,128)(2,1)} %param.9), kind=kOutput, calls=%fused_computation.50 | convolution fusion | flops 135528448 | bytes 2228224 | tf_op jit(solution)/shard_map/dot_general | solution.py:21
  2.8 0.9 %dynamic-slice_convert_fusion = (f32[256]{0:T(256)S(1)}, f32[256]{0:T(256)S(1)}, f32[256]{0:T(256)S(1)}, f32[256]{0:T(256)S(1)}, f32[256]{0:T(256)S(1)}, /*index...) fusion(s32[8192]{0:T(1024)} %param.11, s32[]{:T(128)S(6)} %select_n.93, s32[]{:T(128)S(6)} %select_n.89, ...), kind=kLoop, calls=%fused_computation.128 | loop fusion | flops 2048 | bytes 16416 | tf_op jit(solution)/shard_map/convert_element_type | solution.py:66
  3.7 0.0 copy-start.3
  3.7 0.0 copy-start.4
  3.7 1.6 %fusion.28 = bf16[256,256]{1,0:T(8,128)(2,1)S(1)} fusion(bf16[1024,256]{1,0:T(8,128)(2,1)S(1)} %fusion.18, bf16[1024,256]{1,0:T(8,128)(2,1)} %param.12, bf16[256,256]{1,0:T(8,128)(2,1)} %param.14, bf16[256,256]{1,0:T(8,128)(2,1)} %param.15, f32[256]{0:T(256)S(1)} %get-tuple-element.10), kind=kOutput, calls=%fused_computation.68 | convolution fusion | flops 134742016 | bytes 1442816 | tf_op jit(solution)/shard_map/dot_general | solution.py:26
  5.3 0.6 collective-permute-start.1
  6.0 2.8 %collective-permute-start = (bf16[256,256]{1,0:T(8,128)(2,1)S(1)}, bf16[256,256]{1,0:T(8,128)(2,1)S(1)}, u32[]{:S(2)}, u32[]{:S(2)}) collective-permute-start(bf16[256,256]{1,0:T(8,128)(2,1)S(1)} %fusion.37), channel_id=1, source_target_pairs={{0,1},{1,2},{2,3},{3,4},{4,5},{5,6},{6,7},{7,0},{8,9},{9,10},{10,1... | collective-permute-start | bytes 393224 | tf_op jit(solution)/shard_map/ppermute | solution.py:17
  8.8 0.5 fusion.29
  9.3 4.7 %collective-permute-done = bf16[256,256]{1,0:T(8,128)(2,1)S(1)} collective-permute-done((bf16[256,256]{1,0:T(8,128)(2,1)S(1)}, bf16[256,256]{1,0:T(8,128)(2,1)S(1)}, u32[]{:S(2)}, u32[]{:S(2)}) %collective-permute-start) | collective-permute-done | bytes 131104 | tf_op jit(solution)/shard_map/ppermute | solution.py:17
  14.0 0.4 fusion.19
  14.4 0.0 collective-permute-done.1
  14.4 0.4 fusion.40
  14.8 0.1 collective-permute-start.3
  14.9 0.5 collective-permute-start.2
  15.3 0.5 fusion.30
  15.8 6.6 %collective-permute-done.2 = bf16[256,256]{1,0:T(8,128)(2,1)S(1)} collective-permute-done((bf16[256,256]{1,0:T(8,128)(2,1)S(1)}, bf16[256,256]{1,0:T(8,128)(2,1)S(1)}, u32[]{:S(2)}, u32[]{:S(2)}) %collective-permute-start.2) | collective-permute-done | bytes 131104 | tf_op jit(solution)/shard_map/ppermute | solution.py:17
  22.4 0.4 fusion.20
  22.8 0.3 convolution_divide_fusion.13
  23.1 0.0 collective-permute-done.3
  23.1 0.1 fusion.44
  23.2 0.1 collective-permute-start.5
  23.3 0.1 collective-permute-start.4
  23.4 0.5 fusion.31
  23.9 7.0 %collective-permute-done.4 = bf16[256,256]{1,0:T(8,128)(2,1)S(1)} collective-permute-done((bf16[256,256]{1,0:T(8,128)(2,1)S(1)}, bf16[256,256]{1,0:T(8,128)(2,1)S(1)}, u32[]{:S(2)}, u32[]{:S(2)}) %collective-permute-start.4) | collective-permute-done | bytes 131104 | tf_op jit(solution)/shard_map/ppermute | solution.py:17
  30.9 0.4 fusion.21
  31.2 0.3 convolution_divide_fusion.12
  31.6 0.0 collective-permute-done.5
  31.6 0.1 fusion.48
  31.6 2.0 %collective-permute-start.7 = (bf16[256,256]{1,0:T(8,128)(2,1)S(1)}, bf16[256,256]{1,0:T(8,128)(2,1)S(1)}, u32[]{:S(2)}, u32[]{:S(2)}) collective-permute-start(bf16[256,256]{1,0:T(8,128)(2,1)S(1)} %fusion.48), channel_id=1, source_target_pairs={{0,8},{8,16},{16,24},{24,0},{1,9},{9,17},{17,25},{25,1},{2,10},{10... | collective-permute-start | bytes 393224 | tf_op jit(solution)/shard_map/ppermute | solution.py:17
  33.7 1.5 %collective-permute-start.6 = (bf16[256,256]{1,0:T(8,128)(2,1)S(1)}, bf16[256,256]{1,0:T(8,128)(2,1)S(1)}, u32[]{:S(2)}, u32[]{:S(2)}) collective-permute-start(bf16[256,256]{1,0:T(8,128)(2,1)S(1)} %fusion.49), channel_id=1, source_target_pairs={{0,8},{8,16},{16,24},{24,0},{1,9},{9,17},{17,25},{25,1},{2,10},{10... | collective-permute-start | bytes 393224 | tf_op jit(solution)/shard_map/ppermute | solution.py:17
  35.3 0.5 fusion.32
  35.8 3.9 %collective-permute-done.6 = bf16[256,256]{1,0:T(8,128)(2,1)S(1)} collective-permute-done((bf16[256,256]{1,0:T(8,128)(2,1)S(1)}, bf16[256,256]{1,0:T(8,128)(2,1)S(1)}, u32[]{:S(2)}, u32[]{:S(2)}) %collective-permute-start.6) | collective-permute-done | bytes 131104 | tf_op jit(solution)/shard_map/ppermute | solution.py:17
  39.6 0.4 fusion.22
  40.0 0.3 convolution_divide_fusion.11
  40.4 0.0 collective-permute-done.7
  40.4 0.1 fusion.52
  40.4 0.1 collective-permute-start.9
  40.6 0.1 collective-permute-start.8
  40.6 0.5 fusion.33
  41.1 7.0 %collective-permute-done.8 = bf16[256,256]{1,0:T(8,128)(2,1)S(1)} collective-permute-done((bf16[256,256]{1,0:T(8,128)(2,1)S(1)}, bf16[256,256]{1,0:T(8,128)(2,1)S(1)}, u32[]{:S(2)}, u32[]{:S(2)}) %collective-permute-start.8) | collective-permute-done | bytes 131104 | tf_op jit(solution)/shard_map/ppermute | solution.py:17
  48.1 0.4 fusion.23
  48.5 0.3 convolution_divide_fusion.10
  48.8 0.0 collective-permute-done.9
  48.8 0.1 fusion.56
  48.9 0.1 collective-permute-start.11
  49.0 0.1 collective-permute-start.10
  49.1 0.5 fusion.34
  49.6 7.0 %collective-permute-done.10 = bf16[256,256]{1,0:T(8,128)(2,1)S(1)} collective-permute-done((bf16[256,256]{1,0:T(8,128)(2,1)S(1)}, bf16[256,256]{1,0:T(8,128)(2,1)S(1)}, u32[]{:S(2)}, u32[]{:S(2)}) %collective-permute-start.10) | collective-permute-done | bytes 131104 | tf_op jit(solution)/shard_map/ppermute | solution.py:17
  56.5 0.4 fusion.24
  56.9 0.3 convolution_divide_fusion.9
  57.3 0.0 collective-permute-done.11
  57.3 0.1 fusion.60
  57.3 0.1 collective-permute-start.13
  57.5 0.1 collective-permute-start.12
  57.5 0.5 fusion.35
  58.0 7.0 %collective-permute-done.12 = bf16[256,256]{1,0:T(8,128)(2,1)S(1)} collective-permute-done((bf16[256,256]{1,0:T(8,128)(2,1)S(1)}, bf16[256,256]{1,0:T(8,128)(2,1)S(1)}, u32[]{:S(2)}, u32[]{:S(2)}) %collective-permute-start.12) | collective-permute-done | bytes 131104 | tf_op jit(solution)/shard_map/ppermute | solution.py:17
  65.0 0.4 fusion.25
  65.4 0.3 convolution_divide_fusion.8
  65.7 0.1 fusion.64
  65.8 0.0 copy-start
  65.8 1.7 %fusion.36 = (bf16[1024,256]{1,0:T(8,128)(2,1)}, f32[1024,256]{1,0:T(8,128)}) fusion(bf16[1024,256]{1,0:T(8,128)(2,1)S(1)} %get-tuple-element.24, f32[1024]{0:T(1024)S(1)} %convert_element_type.287, bf16[1024,256]{1,0:T(8,128)(2,1)S(1)} %fusion.25, bf16[256,256]{1,0:T(8,128)(2,1)S(1)} %collective-permute-done.12, f32[1024,256]{1,0:T(8,128)S(1)} %get-tuple-element.25), kind=kOutput, calls=%fused_computation.76 | convolution fusion | flops 136577024 | bytes 3805184 | tf_op jit(solution)/shard_map/dot_general | solution.py:70
  67.5 0.7 %fusion.65 = bf16[256,256]{1,0:T(8,128)(2,1)} fusion(bf16[256,256]{1,0:T(8,128)(2,1)S(1)} %collective-permute-done.12, bf16[256,256]{1,0:T(8,128)(2,1)S(1)} %fusion.64), kind=kLoop, calls=%fused_computation.127 | loop fusion | flops 327680 | bytes 393216 | tf_op jit(solution)/shard_map/convert_element_type | solution.py:32
  (18 shorter events, 0.3 us)
Async XLA Ops:
  0.6 8.1 %copy-start.6 = (bf16[1024,256]{1,0:T(8,128)(2,1)S(1)}, bf16[1024,256]{1,0:T(8,128)(2,1)}, u32[]{:S(2)}) copy-start(bf16[1024,256]{1,0:T(8,128)(2,1)} %param.12) | copy-start | bytes 1572868
  0.6 5.3 %copy-start.1 = (bf16[256,256]{1,0:T(8,128)(2,1)S(1)}, bf16[256,256]{1,0:T(8,128)(2,1)}, u32[]{:S(2)}) copy-start(bf16[256,256]{1,0:T(8,128)(2,1)} %param.14) | copy-start | bytes 393220
  0.7 8.1 %copy-start.2 = (s32[1024]{0:T(1024)S(1)}, s32[1024]{0:T(1024)}, u32[]{:S(2)}) copy-start(s32[1024]{0:T(1024)} %param.10) | copy-start | bytes 12292
  0.7 8.1 %copy-start.5 = (f32[1024,256]{1,0:T(8,128)S(1)}, f32[1024,256]{1,0:T(8,128)}, u32[]{:S(2)}) copy-start(f32[1024,256]{1,0:T(8,128)} %param.13) | copy-start | bytes 3145732
  3.7 10.3 %copy-start.3 = (bf16[1024,2048]{1,0:T(8,128)(2,1)S(1)}, bf16[1024,2048]{1,0:T(8,128)(2,1)}, u32[]{:S(2)}) copy-start(bf16[1024,2048]{1,0:T(8,128)(2,1)} %param.8) | copy-start | bytes 12582916
  3.7 10.3 %copy-start.4 = (bf16[1024,2048]{1,0:T(8,128)(2,1)S(1)}, bf16[1024,2048]{1,0:T(8,128)(2,1)}, u32[]{:S(2)}) copy-start(bf16[1024,2048]{1,0:T(8,128)(2,1)} %param.9) | copy-start | bytes 12582916
  5.3 9.1 %collective-permute-start.1 = (bf16[256,256]{1,0:T(8,128)(2,1)S(1)}, bf16[256,256]{1,0:T(8,128)(2,1)S(1)}, u32[]{:S(2)}, u32[]{:S(2)}) collective-permute-start(bf16[256,256]{1,0:T(8,128)(2,1)S(1)} %fusion.28), channel_id=1, source_target_pairs={{0,1},{1,2},{2,3},{3,4},{4,5},{5,6},{6,7},{7,0},{8,9},{9,10},{10,1... | collective-permute-start | bytes 393224 | tf_op jit(solution)/shard_map/ppermute | solution.py:17
  6.0 8.0 %collective-permute-start = (bf16[256,256]{1,0:T(8,128)(2,1)S(1)}, bf16[256,256]{1,0:T(8,128)(2,1)S(1)}, u32[]{:S(2)}, u32[]{:S(2)}) collective-permute-start(bf16[256,256]{1,0:T(8,128)(2,1)S(1)} %fusion.37), channel_id=1, source_target_pairs={{0,1},{1,2},{2,3},{3,4},{4,5},{5,6},{6,7},{7,0},{8,9},{9,10},{10,1... | collective-permute-start | bytes 393224 | tf_op jit(solution)/shard_map/ppermute | solution.py:17
  14.8 8.4 %collective-permute-start.3 = (bf16[256,256]{1,0:T(8,128)(2,1)S(1)}, bf16[256,256]{1,0:T(8,128)(2,1)S(1)}, u32[]{:S(2)}, u32[]{:S(2)}) collective-permute-start(bf16[256,256]{1,0:T(8,128)(2,1)S(1)} %fusion.40), channel_id=1, source_target_pairs={{0,1},{1,2},{2,3},{3,4},{4,5},{5,6},{6,7},{7,0},{8,9},{9,10},{10,1... | collective-permute-start | bytes 393224 | tf_op jit(solution)/shard_map/ppermute | solution.py:17
  14.9 7.5 %collective-permute-start.2 = (bf16[256,256]{1,0:T(8,128)(2,1)S(1)}, bf16[256,256]{1,0:T(8,128)(2,1)S(1)}, u32[]{:S(2)}, u32[]{:S(2)}) collective-permute-start(bf16[256,256]{1,0:T(8,128)(2,1)S(1)} %fusion.41), channel_id=1, source_target_pairs={{0,1},{1,2},{2,3},{3,4},{4,5},{5,6},{6,7},{7,0},{8,9},{9,10},{10,1... | collective-permute-start | bytes 393224 | tf_op jit(solution)/shard_map/ppermute | solution.py:17
  23.2 8.4 %collective-permute-start.5 = (bf16[256,256]{1,0:T(8,128)(2,1)S(1)}, bf16[256,256]{1,0:T(8,128)(2,1)S(1)}, u32[]{:S(2)}, u32[]{:S(2)}) collective-permute-start(bf16[256,256]{1,0:T(8,128)(2,1)S(1)} %fusion.44), channel_id=1, source_target_pairs={{0,1},{1,2},{2,3},{3,4},{4,5},{5,6},{6,7},{7,0},{8,9},{9,10},{10,1... | collective-permute-start | bytes 393224 | tf_op jit(solution)/shard_map/ppermute | solution.py:17
  23.3 7.5 %collective-permute-start.4 = (bf16[256,256]{1,0:T(8,128)(2,1)S(1)}, bf16[256,256]{1,0:T(8,128)(2,1)S(1)}, u32[]{:S(2)}, u32[]{:S(2)}) collective-permute-start(bf16[256,256]{1,0:T(8,128)(2,1)S(1)} %fusion.45), channel_id=1, source_target_pairs={{0,1},{1,2},{2,3},{3,4},{4,5},{5,6},{6,7},{7,0},{8,9},{9,10},{10,1... | collective-permute-start | bytes 393224 | tf_op jit(solution)/shard_map/ppermute | solution.py:17
  31.6 8.7 %collective-permute-start.7 = (bf16[256,256]{1,0:T(8,128)(2,1)S(1)}, bf16[256,256]{1,0:T(8,128)(2,1)S(1)}, u32[]{:S(2)}, u32[]{:S(2)}) collective-permute-start(bf16[256,256]{1,0:T(8,128)(2,1)S(1)} %fusion.48), channel_id=1, source_target_pairs={{0,8},{8,16},{16,24},{24,0},{1,9},{9,17},{17,25},{25,1},{2,10},{10... | collective-permute-start | bytes 393224 | tf_op jit(solution)/shard_map/ppermute | solution.py:17
  33.7 5.9 %collective-permute-start.6 = (bf16[256,256]{1,0:T(8,128)(2,1)S(1)}, bf16[256,256]{1,0:T(8,128)(2,1)S(1)}, u32[]{:S(2)}, u32[]{:S(2)}) collective-permute-start(bf16[256,256]{1,0:T(8,128)(2,1)S(1)} %fusion.49), channel_id=1, source_target_pairs={{0,8},{8,16},{16,24},{24,0},{1,9},{9,17},{17,25},{25,1},{2,10},{10... | collective-permute-start | bytes 393224 | tf_op jit(solution)/shard_map/ppermute | solution.py:17
  40.4 8.4 %collective-permute-start.9 = (bf16[256,256]{1,0:T(8,128)(2,1)S(1)}, bf16[256,256]{1,0:T(8,128)(2,1)S(1)}, u32[]{:S(2)}, u32[]{:S(2)}) collective-permute-start(bf16[256,256]{1,0:T(8,128)(2,1)S(1)} %fusion.52), channel_id=1, source_target_pairs={{0,1},{1,2},{2,3},{3,4},{4,5},{5,6},{6,7},{7,0},{8,9},{9,10},{10,1... | collective-permute-start | bytes 393224 | tf_op jit(solution)/shard_map/ppermute | solution.py:17
  40.6 7.5 %collective-permute-start.8 = (bf16[256,256]{1,0:T(8,128)(2,1)S(1)}, bf16[256,256]{1,0:T(8,128)(2,1)S(1)}, u32[]{:S(2)}, u32[]{:S(2)}) collective-permute-start(bf16[256,256]{1,0:T(8,128)(2,1)S(1)} %fusion.53), channel_id=1, source_target_pairs={{0,1},{1,2},{2,3},{3,4},{4,5},{5,6},{6,7},{7,0},{8,9},{9,10},{10,1... | collective-permute-start | bytes 393224 | tf_op jit(solution)/shard_map/ppermute | solution.py:17
  48.9 8.4 %collective-permute-start.11 = (bf16[256,256]{1,0:T(8,128)(2,1)S(1)}, bf16[256,256]{1,0:T(8,128)(2,1)S(1)}, u32[]{:S(2)}, u32[]{:S(2)}) collective-permute-start(bf16[256,256]{1,0:T(8,128)(2,1)S(1)} %fusion.56), channel_id=1, source_target_pairs={{0,1},{1,2},{2,3},{3,4},{4,5},{5,6},{6,7},{7,0},{8,9},{9,10},{10,1... | collective-permute-start | bytes 393224 | tf_op jit(solution)/shard_map/ppermute | solution.py:17
  49.0 7.5 %collective-permute-start.10 = (bf16[256,256]{1,0:T(8,128)(2,1)S(1)}, bf16[256,256]{1,0:T(8,128)(2,1)S(1)}, u32[]{:S(2)}, u32[]{:S(2)}) collective-permute-start(bf16[256,256]{1,0:T(8,128)(2,1)S(1)} %fusion.57), channel_id=1, source_target_pairs={{0,1},{1,2},{2,3},{3,4},{4,5},{5,6},{6,7},{7,0},{8,9},{9,10},{10,1... | collective-permute-start | bytes 393224 | tf_op jit(solution)/shard_map/ppermute | solution.py:17
  57.3 8.4 %collective-permute-start.13 = (bf16[256,256]{1,0:T(8,128)(2,1)S(1)}, bf16[256,256]{1,0:T(8,128)(2,1)S(1)}, u32[]{:S(2)}, u32[]{:S(2)}) collective-permute-start(bf16[256,256]{1,0:T(8,128)(2,1)S(1)} %fusion.60), channel_id=1, source_target_pairs={{0,1},{1,2},{2,3},{3,4},{4,5},{5,6},{6,7},{7,0},{8,9},{9,10},{10,1... | collective-permute-start | bytes 393224 | tf_op jit(solution)/shard_map/ppermute | solution.py:17
  57.5 7.5 %collective-permute-start.12 = (bf16[256,256]{1,0:T(8,128)(2,1)S(1)}, bf16[256,256]{1,0:T(8,128)(2,1)S(1)}, u32[]{:S(2)}, u32[]{:S(2)}) collective-permute-start(bf16[256,256]{1,0:T(8,128)(2,1)S(1)} %fusion.61), channel_id=1, source_target_pairs={{0,1},{1,2},{2,3},{3,4},{4,5},{5,6},{6,7},{7,0},{8,9},{9,10},{10,1... | collective-permute-start | bytes 393224 | tf_op jit(solution)/shard_map/ppermute | solution.py:17
  65.8 2.4 %copy-start = (bf16[256,256]{1,0:T(8,128)(2,1)}, bf16[256,256]{1,0:T(8,128)(2,1)S(1)}, u32[]{:S(2)}) copy-start(bf16[256,256]{1,0:T(8,128)(2,1)S(1)} %fusion.64) | copy-start | bytes 393220
where the time goes:
time: 68.4 us; the launch traced here: 68.2 us
  waiting for transfers between devices  43.1 us (63%)
  matrix products  13.6 us (20%)
  starting transfers between devices  7.89 us (12%)
  other arithmetic  2.34 us (3%)
  between operations  1.22 us (2%)
    ppermute x14, waiting for transfers between devices, shifted(): return lax.ppermute(value, axis, pairs)  43.1 us
    ppermute x14, starting transfers between devices, shifted(): return lax.ppermute(value, axis, pairs)  7.89 us
    dot_general x8, matrix products, body(): grad_sum = jnp.dot(misfit, items, preferred_element_type=jnp.float32)  5.15 us
    dot_general x8, matrix products, misfit_of(): predicted = jnp.dot(users, items.T, preferred_element_type=jnp.float32)  4.48 us
    dot_general x8, matrix products, item_step(): lax.dot_general(misfit, users, (((0,), (0,)), ((), ())), preferred_elemen...  4 us
  transfers between devices with their start and end apart: 14, of which 7 were waited for; matrix products, arithmetic and copies ran while one was open for 12% of the time, Pallas kernels for 0%

commit v1 on v0

v1 whole, which is shorter than its diff:
```python
import functools

import jax
import jax.numpy as jnp
from jax import lax
from jax.experimental import pallas as pl
from jax.experimental.pallas import tpu as pltpu
from jax.sharding import PartitionSpec as P

STEPS = 8
CHUNKS = 2
TILE = 256
LANES = 128
MESH = pl.DeviceIdType.MESH

learn_rate = 0.3
moment_rate = 0.9
decay_rate = 0.02


def kernel(
    n_outer, n_inner,
    x_hbm, w_hbm, uc_hbm, ic_hbm, u_hbm, p_hbm, v_hbm, q_hbm,
    u_out, p_out, v_out, q_out,
    x, w, uc, ic, u, ut, p, v0, q0, vt, qt, vn, qn, mis, rcu, counts,
    x_sem, w_sem, in_sem, send_sem, recv_sem, out_sem,
):
    outer = lax.axis_index("outer")
    inner = lax.axis_index("inner")
    i_right, i_left = lax.rem(inner + 1, n_inner), lax.rem(inner + n_inner - 1, n_inner)
    o_right, o_left = lax.rem(outer + 1, n_outer), lax.rem(outer + n_outer - 1, n_outer)

    users, rank = u.shape
    block = v0.shape[0]
    part = block // CHUNKS
    tile = min(TILE, users)

    def load(src, dst, sem):
        copy = pltpu.make_async_copy(src, dst, sem)
        copy.start()
        return copy

    v_load = load(v_hbm, v0, in_sem.at[0])
    u_load = load(u_hbm, u, in_sem.at[1])
    loads = []
    for s in range(STEPS):
        cols = slice(s * block, (s + 1) * block)
        loads.append((
            load(x_hbm.at[:, cols], x.at[s], x_sem.at[s]),
            load(w_hbm.at[:, cols], w.at[s], w_sem.at[s]),
        ))
        if s == 0:
            q_load = load(q_hbm, q0, in_sem.at[2])
            ic_load = load(ic_hbm, ic, in_sem.at[3])
            uc_load = load(uc_hbm, uc, in_sem.at[4])
            p_load = load(p_hbm, p, in_sem.at[5])

    barrier = pltpu.get_barrier_semaphore()
    for where in ((outer, i_left), (outer, i_right), (o_left, inner), (o_right, inner)):
        pl.semaphore_signal(barrier, inc=1, device_id=where, device_id_type=MESH)

    v_load.wait()
    vt[0] = v0[...].T
    u_load.wait()
    for t in range(users // tile):
        rows = slice(t * tile, (t + 1) * tile)
        ut[:, rows] = u[rows, :].T
    q_load.wait()
    qt[0] = q0[...].T

    ic_load.wait()
    per = block // LANES
    for s in range(STEPS):
        late = 1 if s >= STEPS // 2 else 0
        o_from = lax.rem(outer - late + n_outer, n_outer)
        i_from = lax.rem(inner - (s - late) + n_inner * STEPS, n_inner)
        first = (o_from * n_inner + i_from) * per
        for j in range(per):
            row = ic[pl.ds(first + j, 1), :].astype(jnp.float32)
            counts[s : s + 1, j * LANES : (j + 1) * LANES] = 1.0 / row
    uc_load.wait()
    flipped = (1.0 / uc[...].astype(jnp.float32)).T
    for j in range(users // LANES):
        rcu[j * LANES : (j + 1) * LANES, :] = jnp.broadcast_to(flipped[:, j : j + 1], (LANES, LANES))

    sends = []
    outs = []
    arrivals = [None]
    for s in range(STEPS):
        last = s == STEPS - 1
        if s == STEPS // 2 - 1:
            target = (o_right, inner)
        else:
            target = (outer, i_right)
        if s == 0:
            loads[0][0].wait()
            loads[0][1].wait()
        else:
            loads[s][0].wait()
            loads[s][1].wait()
        copies = []
        for k in range(CHUNKS):
            cols = slice(k * part, (k + 1) * part)
            if s > 0:
                arrivals[s][k][0].wait_recv()
            items = vt[s, :, cols]
            for t in range(users // tile):
                rows = slice(t * tile, (t + 1) * tile)
                pred = jnp.dot(u[rows, :], items, preferred_element_type=jnp.float32)
                rated = x[s, rows, cols].astype(jnp.float32)
                weight = w[s, rows, cols].astype(jnp.float32)
                mis[rows, cols] = (weight * (pred - rated)).astype(jnp.bfloat16)
            product = jnp.dot(ut[...], mis[:, cols], preferred_element_type=jnp.float32)
            if s > 0:
                arrivals[s][k][1].wait_recv()
            old = items.astype(jnp.float32)
            grad = product * counts[s : s + 1, cols] + decay_rate * old
            moment = (moment_rate * qt[s, :, cols].astype(jnp.float32) + grad).astype(jnp.bfloat16)
            qn[s, :, cols] = moment
            vn[s, :, cols] = (old - learn_rate * moment.astype(jnp.float32)).astype(jnp.bfloat16)
            if not last:
                if s == 0 and k == 0:
                    pl.semaphore_wait(barrier, 4)
                pair = []
                for j, (src, dst) in enumerate(((vn, vt), (qn, qt))):
                    copy = pltpu.make_async_remote_copy(
                        src_ref=src.at[s, :, cols],
                        dst_ref=dst.at[s + 1, :, cols],
                        send_sem=send_sem.at[s, k, j],
                        recv_sem=recv_sem.at[s, k, j],
                        device_id=target,
                        device_id_type=MESH,
                    )
                    copy.start()
                    pair.append(copy)
                copies.append(pair)
            else:
                v0[cols, :] = vn[s, :, cols].T
                q0[cols, :] = qn[s, :, cols].T
                for j, (src, dst) in enumerate(((v0, v_out), (q0, q_out))):
                    outs.append(load(src.at[cols], dst.at[cols], out_sem.at[0, 2 * k + j]))
        arrivals.append(copies)
        sends.append(copies)
        if s == 0:
            p_load.wait()
        for t in range(users // tile):
            rows = slice(t * tile, (t + 1) * tile)
            total = lax.dot_general(
                mis[rows, :], vt[s], (((1,), (1,)), ((), ())), preferred_element_type=jnp.float32
            )
            old = u[rows, :].astype(jnp.float32)
            scale = jnp.concatenate([rcu[rows, :]] * (rank // LANES), axis=1)
            moment = moment_rate * p[rows, :] + (total * scale + decay_rate * old)
            p[rows, :] = moment
            new = (old - learn_rate * moment).astype(jnp.bfloat16)
            u[rows, :] = new
            if last:
                outs.append(load(u.at[rows], u_out.at[rows], out_sem.at[1, t]))
                outs.append(load(p.at[rows], p_out.at[rows], out_sem.at[2, t]))
            else:
                ut[:, rows] = new.T
    for copies in sends:
        for pair in copies:
            for copy in pair:
                copy.wait_send()
    for copy in outs:
        copy.wait()


def body(ratings, rating_weights, user_counts, item_counts, users, user_moment, items, item_moment):
    n_outer = lax.axis_size("outer")
    n_inner = lax.axis_size("inner")
    n_users, rank = users.shape
    block = items.shape[0]
    n_items = item_counts.shape[0]
    tiles = max(n_users // min(TILE, n_users), 2 * CHUNKS)
    bf16, f32, i32 = jnp.bfloat16, jnp.float32, jnp.int32
    return pl.pallas_call(
        functools.partial(kernel, n_outer, n_inner),
        out_shape=(
            jax.ShapeDtypeStruct(users.shape, bf16),
            jax.ShapeDtypeStruct(user_moment.shape, f32),
            jax.ShapeDtypeStruct(items.shape, bf16),
            jax.ShapeDtypeStruct(item_moment.shape, bf16),
        ),
        in_specs=[pl.BlockSpec(memory_space=pltpu.HBM)] * 8,
        out_specs=(pl.BlockSpec(memory_space=pl.ANY),) * 4,
        scratch_shapes=[
            pltpu.VMEM((STEPS, n_users, block), bf16),
            pltpu.VMEM((STEPS, n_users, block), bf16),
            pltpu.VMEM((n_users // LANES, LANES), i32),
            pltpu.VMEM((n_items // LANES, LANES), i32),
            pltpu.VMEM((n_users, rank), bf16),
            pltpu.VMEM((rank, n_users), bf16),
            pltpu.VMEM((n_users, rank), f32),
            pltpu.VMEM((block, rank), bf16),
            pltpu.VMEM((block, rank), bf16),
            pltpu.VMEM((STEPS, rank, block), bf16),
            pltpu.VMEM((STEPS, rank, block), bf16),
            pltpu.VMEM((STEPS, rank, block), bf16),
            pltpu.VMEM((STEPS, rank, block), bf16),
            pltpu.VMEM((n_users, block), bf16),
            pltpu.VMEM((n_users, LANES), f32),
            pltpu.VMEM((STEPS, block), f32),
            pltpu.SemaphoreType.DMA((STEPS,)),
            pltpu.SemaphoreType.DMA((STEPS,)),
            pltpu.SemaphoreType.DMA((6,)),
            pltpu.SemaphoreType.DMA((STEPS, CHUNKS, 2)),
            pltpu.SemaphoreType.DMA((STEPS, CHUNKS, 2)),
            pltpu.SemaphoreType.DMA((3, tiles)),
        ],
        compiler_params=pltpu.CompilerParams(
            collective_id=0, has_side_effects=True, vmem_limit_bytes=48 * 1024 * 1024
        ),
    )(
        ratings,
        rating_weights,
        user_counts.reshape(n_users // LANES, LANES),
        item_counts.reshape(n_items // LANES, LANES),
        users,
        user_moment,
        items,
        item_moment,
    )


def solution(mesh):
    spread = P(("outer", "inner"), None)
    in_specs = (spread, spread, P(("outer", "inner")), P(), spread, spread, spread, spread)
    return jax.shard_map(
        body, mesh=mesh, in_specs=in_specs, out_specs=(spread,) * 4, check_vma=False
    )
```

time: 68.4 us -> 43.1 us (0.63)
  waiting for transfers between devices: 43.1 us -> 0 us
  Pallas kernels: 0 us -> 33.5 us
  matrix products: 13.6 us -> 0 us
  local copies, waits for them, and re-layouts: 0.04 us -> 8.58 us
  starting transfers between devices: 7.89 us -> 0 us
  other arithmetic: 2.34 us -> 0 us
    ppermute x14 -> x0, waiting for transfers between devices: 43.1 us -> none  [shifted(): return lax.ppermute(value, axis, pairs)]
    pallas_call x0 -> x1, Pallas kernels: none -> 33.5 us  [body(): pl.pallas_call(functools.partial(kernel, n_outer, n_inner), out_shape=(ja...]
    dot_general x24 -> x0, matrix products: 13.6 us -> none  [the longest x8 5.15 us: body(): grad_sum = jnp.dot(misfit, items, preferred_element_type=jnp.float32)]
    unnamed x14 -> x16, local copies, waits for them, and re-layouts: 0.04 us -> 8.58 us
    ppermute x14 -> x0, starting transfers between devices: 7.89 us -> none  [shifted(): return lax.ppermute(value, axis, pairs)]
    convert_element_type x16 -> x0, other arithmetic: 2.34 us -> none  [the longest x8 1.01 us: item_step(): (items.astype(jnp.float32) - learn_rate * kept.astype(jnp.float32)).astyp...]
  transfers between devices with their start and end apart: 14 -> 0, of which waited for: 7 -> 0; matrix products, arithmetic and copies ran while one was open for 12% -> 0% of each run, Pallas kernels for 0% -> 0%
where the time goes in v1:
time: 43.1 us; the launch traced here: 42.8 us
  Pallas kernels  33.5 us (78%)
  local copies, waits for them, and re-layouts  8.58 us (20%)
  between operations  0.66 us (2%)
    pallas_call x1, Pallas kernels, body(): pl.pallas_call(functools.partial(kernel, n_outer, n_inner), out_shape=(ja...  33.5 us
    unnamed x16, local copies, waits for them, and re-layouts  8.58 us

profile of v1, /device:TPU:0, one launch (start us, length us, event | category | flops | bytes accessed | tf_op | source)
XLA Modules:
  0.0 42.8 jit_solution(9410067712837383733)
XLA Ops:
  0.6 0.0 copy-start
  0.6 1.2 %copy-done = f32[1024,256]{1,0:T(8,128)S(1)} copy-done((f32[1024,256]{1,0:T(8,128)S(1)}, f32[1024,256]{1,0:T(8,128)}, u32[]{:S(2)}) %copy-start) | copy-done | bytes 1048600
  1.9 0.0 copy-start.1
  1.9 1.0 %copy-done.1 = bf16[1024,256]{1,0:T(8,128)(2,1)S(1)} copy-done((bf16[1024,256]{1,0:T(8,128)(2,1)S(1)}, bf16[1024,256]{1,0:T(8,128)(2,1)}, u32[]{:S(2)}) %copy-start.1) | copy-done | bytes 524312
  2.9 0.0 copy-start.2
  2.9 0.9 %copy-done.2 = bf16[256,256]{1,0:T(8,128)(2,1)S(1)} copy-done((bf16[256,256]{1,0:T(8,128)(2,1)S(1)}, bf16[256,256]{1,0:T(8,128)(2,1)}, u32[]{:S(2)}) %copy-start.2) | copy-done | bytes 131096
  3.8 0.0 copy-start.3
  3.8 0.9 %copy-done.3 = bf16[256,256]{1,0:T(8,128)(2,1)S(1)} copy-done((bf16[256,256]{1,0:T(8,128)(2,1)S(1)}, bf16[256,256]{1,0:T(8,128)(2,1)}, u32[]{:S(2)}) %copy-start.3) | copy-done | bytes 131096
  4.7 0.0 copy-start.4
  4.7 0.8 %copy-done.4 = s32[8192]{0:T(1024)S(1)} copy-done((s32[8192]{0:T(1024)S(1)}, s32[8192]{0:T(1024)}, u32[]{:S(2)}) %copy-start.4) | copy-done | bytes 32792
  5.5 0.0 copy-start.5
  5.5 0.7 %copy-done.5 = s32[1024]{0:T(1024)S(1)} copy-done((s32[1024]{0:T(1024)S(1)}, s32[1024]{0:T(1024)}, u32[]{:S(2)}) %copy-start.5) | copy-done | bytes 4120
  6.2 33.5 %shard_map.111 = (bf16[1024,256]{1,0:T(8,128)(2,1)S(1)}, f32[1024,256]{1,0:T(8,128)S(1)}, bf16[256,256]{1,0:T(8,128)(2,1)S(1)}, bf16[256,256]{1,0:T(8,128)(2,1)S(1)}) custom-call(bf16[1024,2048]{1,0:T(8,128)(2,1)} %x_hbm.1, bf16[1024,2048]{1,0:T(8,128)(2,1)} %w_hbm.1, s32[8,128]{1,0:T(8,128)S(1)} %bitcast.3, s32[64,128]{1,0:T(8,128)S(1)} %bitcast.2, ...), custom_call_target="tpu_custom_call" | custom-call | tf_op jit(solution)/shard_map/pallas_call | solution.py:178
  39.7 0.8 %copy.16 = bf16[1024,256]{1,0:T(8,128)(2,1)} copy(bf16[1024,256]{1,0:T(8,128)(2,1)S(1)} %get-tuple-element.8) | data formatting | bytes 1048576
  40.5 1.0 %copy.17 = f32[1024,256]{1,0:T(8,128)} copy(f32[1024,256]{1,0:T(8,128)S(1)} %get-tuple-element.9) | data formatting | bytes 2097152
  41.5 0.7 %copy.18 = bf16[256,256]{1,0:T(8,128)(2,1)} copy(bf16[256,256]{1,0:T(8,128)(2,1)S(1)} %get-tuple-element.10) | data formatting | bytes 262144
  42.1 0.7 %copy.19 = bf16[256,256]{1,0:T(8,128)(2,1)} copy(bf16[256,256]{1,0:T(8,128)(2,1)S(1)} %get-tuple-element.11) | data formatting | bytes 262144
Async XLA Ops:
  0.6 1.2 %copy-start = (f32[1024,256]{1,0:T(8,128)S(1)}, f32[1024,256]{1,0:T(8,128)}, u32[]{:S(2)}) copy-start(f32[1024,256]{1,0:T(8,128)} %p_hbm.1) | copy-start | bytes 3145732
  1.9 1.0 %copy-start.1 = (bf16[1024,256]{1,0:T(8,128)(2,1)S(1)}, bf16[1024,256]{1,0:T(8,128)(2,1)}, u32[]{:S(2)}) copy-start(bf16[1024,256]{1,0:T(8,128)(2,1)} %u_hbm.1) | copy-start | bytes 1572868
  2.9 0.9 %copy-start.2 = (bf16[256,256]{1,0:T(8,128)(2,1)S(1)}, bf16[256,256]{1,0:T(8,128)(2,1)}, u32[]{:S(2)}) copy-start(bf16[256,256]{1,0:T(8,128)(2,1)} %v_hbm.1) | copy-start | bytes 393220
  3.8 0.9 %copy-start.3 = (bf16[256,256]{1,0:T(8,128)(2,1)S(1)}, bf16[256,256]{1,0:T(8,128)(2,1)}, u32[]{:S(2)}) copy-start(bf16[256,256]{1,0:T(8,128)(2,1)} %q_hbm.1) | copy-start | bytes 393220
  4.7 0.8 %copy-start.4 = (s32[8192]{0:T(1024)S(1)}, s32[8192]{0:T(1024)}, u32[]{:S(2)}) copy-start(s32[8192]{0:T(1024)} %param.11) | copy-start | bytes 98308
  5.5 0.7 %copy-start.5 = (s32[1024]{0:T(1024)S(1)}, s32[1024]{0:T(1024)}, u32[]{:S(2)}) copy-start(s32[1024]{0:T(1024)} %param.10) | copy-start | bytes 12292
